TPU v7x, 32 devices: a whole 2x2x4 slice. The times are simulated.
32 devices in a mesh: groups: 2 (over x), blk: 8 (over z, y), rows: 2 (over core).
Axes of the slice: x: 2, y: 2, z: 4, core: 2. Of those that a mesh axis runs over, the one named last changes fastest.
Arguments:
- features: bfloat16 [8, 16, 256, 512], P('groups', 'rows', 'blk'), parts along dimension 0, may hold values from -60 to 60
- gain_in: float32 [512], replicated, may hold values from 0.25 to 1.75
- shift_in: float32 [512], replicated, may hold values from -3 to 3
- conv_first: bfloat16 [3, 3, 512, 256], replicated, may hold values from -0.09375 to 0.09375
- bias_first: float32 [256], replicated, may hold values from -3 to 3
- short_weight: bfloat16 [512, 256], replicated, may hold values from -0.25 to 0.25
- short_bias: float32 [256], replicated, may hold values from -3 to 3
- gains_rest: float32 [5, 256], replicated, may hold values from 0.25 to 1.75
- shifts_rest: float32 [5, 256], replicated, may hold values from -3 to 3
- convs_rest: bfloat16 [5, 3, 3, 256, 256], replicated, may hold values from -0.125 to 0.125
- biases_rest: float32 [5, 256], replicated, may hold values from -3 to 3
Outputs:
- decoded: bfloat16 [8, 16, 256, 256], P('groups', 'rows', 'blk'), parts along dimension 0
There are 2 independent parts, one for each index of `groups`. A program takes and returns all parts, laid end to end along the dimension named above; an argument that names none is the same for every part. Nothing has to cross between parts.
All inputs are finite; a program needn't handle non-finite values.
Results may differ from a plain program's by a relative error of at most 0.0065.
Values may be sent and summed in bfloat16 or wider, within the bound.
A program may use at most 128 MiB of HBM per device.

v0:
```python
import jax
import jax.numpy as jnp
from jax import lax
from jax.sharding import PartitionSpec as P

GROUPS = 32
RESNETS = 3


EPS = 1e-06


def with_halo(block, sides, width, periodic):
    for axis, dim in sides:
        count = lax.axis_size(axis)
        forward = [(i, i + 1) for i in range(count - 1)]
        if periodic:
            forward.append((count - 1, 0))
        backward = [(target, source) for source, target in forward]
        low = lax.ppermute(
            lax.slice_in_dim(block, block.shape[dim] - width, None, axis=dim), axis, forward
        )
        high = lax.ppermute(lax.slice_in_dim(block, 0, width, axis=dim), axis, backward)
        block = jnp.concatenate([low, block, high], axis=dim)
    return block


def group_totals(values, groups):
    shaped = values.reshape(values.shape[0], -1, groups, values.shape[3] // groups)
    return jnp.sum(shaped, axis=(1, 3))


def per_channel(stat, channels):
    return jnp.repeat(stat, channels // stat.shape[1], axis=1)[:, None, None, :]


def norm_act(values, inner, gain, shift):
    channels = values.shape[3]
    count = (
        inner.shape[1]
        * inner.shape[2]
        * lax.axis_size("blk")
        * lax.axis_size("rows")
        * (channels // GROUPS)
    )
    total, square = lax.psum(
        (group_totals(inner, GROUPS), group_totals(inner * inner, GROUPS)), ("blk", "rows")
    )
    center = total / count
    spread = square / count - center * center
    scaled = (values - per_channel(center, channels)) * per_channel(
        lax.rsqrt(spread + EPS), channels
    ) * gain + shift
    return scaled * jax.nn.sigmoid(scaled)


def convolve(padded, weight, bias):
    height = padded.shape[1] - 2
    width = padded.shape[2] - 2
    inputs = weight.shape[2]
    total = jnp.zeros((padded.shape[0] * height * width, weight.shape[3]), jnp.float32)
    for shift_row in range(3):
        band = padded[:, shift_row : shift_row + height]
        stacked = jnp.concatenate(
            [band[:, :, shift_col : shift_col + width] for shift_col in range(3)], axis=3
        )
        total = total + jnp.dot(
            stacked.reshape(-1, 3 * inputs),
            weight[shift_row].reshape(3 * inputs, weight.shape[3]),
            preferred_element_type=jnp.float32,
        )
    return total.reshape(padded.shape[0], height, width, weight.shape[3]) + bias


def extend_once(field):
    tall = with_halo(field, (("rows", 1),), 1, False)
    return with_halo(tall, (("blk", 2),), 1, True)


def body(
    features,
    gain_in,
    shift_in,
    conv_first,
    bias_first,
    short_weight,
    short_bias,
    gains_rest,
    shifts_rest,
    convs_rest,
    biases_rest,
):
    stream = features
    for block in range(RESNETS):
        if block == 0:
            first = (gain_in, shift_in, conv_first, bias_first)
        else:
            first = (
                gains_rest[2 * block - 1],
                shifts_rest[2 * block - 1],
                convs_rest[2 * block - 1],
                biases_rest[2 * block - 1],
            )
        second = (
            gains_rest[2 * block],
            shifts_rest[2 * block],
            convs_rest[2 * block],
            biases_rest[2 * block],
        )
        source = stream.astype(jnp.float32)
        active = norm_act(source, source, first[0], first[1]).astype(jnp.bfloat16)
        inner = convolve(extend_once(active), first[2], first[3]).astype(jnp.bfloat16)
        middle = inner.astype(jnp.float32)
        active_two = norm_act(middle, middle, second[0], second[1]).astype(jnp.bfloat16)
        branch = convolve(extend_once(active_two), second[2], second[3])
        if block == 0:
            flat = stream.reshape(-1, stream.shape[3])
            skip = jnp.dot(flat, short_weight, preferred_element_type=jnp.float32) + short_bias
            skip = skip.reshape(
                stream.shape[0], stream.shape[1], stream.shape[2], short_weight.shape[1]
            )
        else:
            skip = stream.astype(jnp.float32)
        stream = (skip + branch).astype(jnp.bfloat16)
    return stream


def solution(mesh):
    placed = (P("groups", "rows", "blk", None), P(), P(), P(), P(), P(), P(), P(), P(), P(), P())
    return jax.shard_map(
        body,
        mesh=mesh,
        in_specs=placed,
        out_specs=P("groups", "rows", "blk", None),
        check_vma=False,
    )
```

profile of v0, /device:TPU:0, one launch (start us, length us, event | category | flops | bytes accessed | tf_op | source)
XLA Modules:
  0.0 329.6 jit_solution(16887478936183795066)
XLA Ops:
  2.0 35.0 %all-reduce.5 = (f32[4,32]{1,0:T(4,128)S(1)}, f32[4,32]{1,0:T(4,128)S(1)}) all-reduce(f32[4,32]{1,0:T(4,128)S(1)} %reduce_sum.127, f32[4,32]{1,0:T(4,128)S(1)} %reduce_sum.124), channel_id=1, replica_groups=mesh['groups'=2,'blk'=8,'rows'=2] {'blk','rows'}, use_global_device_ids=true, to_apply=%region_5.0 | all-reduce | flops 256 | bytes 2048 | tf_op jit(solution)/shard_map/psum | solution.py:46
  41.0 2.9 fusion.68
  44.0 2.6 fusion.67
  47.4 4.7 %collective-permute-start.3 = (bf16[4,10,1,512]{3,2,1,0:T(2,128)(2,1)S(1)}, bf16[4,10,1,512]{3,2,1,0:T(2,128)(2,1)}, u32[]{:S(2)}, u32[]{:S(2)}) collective-permute-start(bf16[4,10,1,512]{3,2,1,0:T(2,128)(2,1)S(1)} %get-tuple-element.65), channel_id=1, source_target_pairs={{2,0},{4,2},{6,4},{8,6},{10,8},{12,10},{14,12},{0,14},{3,1},{5,3},... | collective-permute-start | bytes 122888 | tf_op jit(solution)/shard_map/ppermute | solution.py:23
  52.2 3.3 %collective-permute-done.2 = bf16[4,10,1,512]{3,2,1,0:T(2,128)(2,1)} collective-permute-done((bf16[4,10,1,512]{3,2,1,0:T(2,128)(2,1)}, bf16[4,10,1,512]{3,2,1,0:T(2,128)(2,1)}, u32[]{:S(2)}, u32[]{:S(2)}) %collective-permute-start.2) | collective-permute-done | bytes 40992 | tf_op jit(solution)/shard_map/ppermute | solution.py:20
  66.4 33.6 %all-reduce.4 = (f32[4,32]{1,0:T(4,128)S(1)}, f32[4,32]{1,0:T(4,128)S(1)}) all-reduce(f32[4,32]{1,0:T(4,128)S(1)} %copy.38, f32[4,32]{1,0:T(4,128)S(1)} %copy.37), channel_id=1, replica_groups=mesh['groups'=2,'blk'=8,'rows'=2] {'blk','rows'}, use_global_device_ids=true, to_apply=%region_9.0 | all-reduce | flops 256 | bytes 2048 | tf_op jit(solution)/shard_map/psum | solution.py:46
  105.4 4.7 %collective-permute-start.7 = (bf16[4,10,1,256]{3,2,1,0:T(2,128)(2,1)S(1)}, bf16[4,10,1,256]{3,2,1,0:T(2,128)(2,1)S(1)}, u32[]{:S(2)}, u32[]{:S(2)}) collective-permute-start(bf16[4,10,1,256]{3,2,1,0:T(2,128)(2,1)S(1)} %get-tuple-element.120), channel_id=1, source_target_pairs={{2,0},{4,2},{6,4},{8,6},{10,8},{12,10},{14,12},{0,14},{3,1},{5,3},... | collective-permute-start | bytes 61448 | tf_op jit(solution)/shard_map/ppermute | solution.py:23
  118.1 3.0 convert_reduce_fusion.1
  121.3 32.5 %all-reduce.3 = (f32[4,32]{1,0:T(4,128)S(1)}, f32[4,32]{1,0:T(4,128)S(1)}) all-reduce(f32[4,32]{1,0:T(4,128)S(1)} %copy.42, f32[4,32]{1,0:T(4,128)S(1)} %copy.41), channel_id=1, replica_groups=mesh['groups'=2,'blk'=8,'rows'=2] {'blk','rows'}, use_global_device_ids=true, to_apply=%region_13.0 | all-reduce | flops 256 | bytes 2048 | tf_op jit(solution)/shard_map/psum | solution.py:46
  158.1 1.8 collective-permute-done.9
  160.0 4.7 %collective-permute-start.11 = (bf16[4,10,1,256]{3,2,1,0:T(2,128)(2,1)S(1)}, bf16[4,10,1,256]{3,2,1,0:T(2,128)(2,1)S(1)}, u32[]{:S(2)}, u32[]{:S(2)}) collective-permute-start(bf16[4,10,1,256]{3,2,1,0:T(2,128)(2,1)S(1)} %get-tuple-element.116), channel_id=1, source_target_pairs={{2,0},{4,2},{6,4},{8,6},{10,8},{12,10},{14,12},{0,14},{3,1},{5,3},... | collective-permute-start | bytes 61448 | tf_op jit(solution)/shard_map/ppermute | solution.py:23
  164.8 1.9 collective-permute-done.10
  174.9 32.5 %all-reduce.2 = (f32[4,32]{1,0:T(4,128)S(1)}, f32[4,32]{1,0:T(4,128)S(1)}) all-reduce(f32[4,32]{1,0:T(4,128)S(1)} %copy.45, f32[4,32]{1,0:T(4,128)S(1)} %copy.44), channel_id=1, replica_groups=mesh['groups'=2,'blk'=8,'rows'=2] {'blk','rows'}, use_global_device_ids=true, to_apply=%region_17.0 | all-reduce | flops 256 | bytes 2048 | tf_op jit(solution)/shard_map/psum | solution.py:46
  210.8 1.8 collective-permute-done.13
  212.8 4.7 %collective-permute-start.15 = (bf16[4,10,1,256]{3,2,1,0:T(2,128)(2,1)S(1)}, bf16[4,10,1,256]{3,2,1,0:T(2,128)(2,1)S(1)}, u32[]{:S(2)}, u32[]{:S(2)}) collective-permute-start(bf16[4,10,1,256]{3,2,1,0:T(2,128)(2,1)S(1)} %get-tuple-element.112), channel_id=1, source_target_pairs={{2,0},{4,2},{6,4},{8,6},{10,8},{12,10},{14,12},{0,14},{3,1},{5,3},... | collective-permute-start | bytes 61448 | tf_op jit(solution)/shard_map/ppermute | solution.py:23
  217.6 1.9 collective-permute-done.14
  227.9 32.5 %all-reduce.1 = (f32[4,32]{1,0:T(4,128)S(1)}, f32[4,32]{1,0:T(4,128)S(1)}) all-reduce(f32[4,32]{1,0:T(4,128)S(1)} %copy.48, f32[4,32]{1,0:T(4,128)S(1)} %copy.47), channel_id=1, replica_groups=mesh['groups'=2,'blk'=8,'rows'=2] {'blk','rows'}, use_global_device_ids=true, to_apply=%region_21.0 | all-reduce | flops 256 | bytes 2048 | tf_op jit(solution)/shard_map/psum | solution.py:46
  264.6 1.8 collective-permute-done.17
  266.6 4.7 %collective-permute-start.19 = (bf16[4,10,1,256]{3,2,1,0:T(2,128)(2,1)S(1)}, bf16[4,10,1,256]{3,2,1,0:T(2,128)(2,1)S(1)}, u32[]{:S(2)}, u32[]{:S(2)}) collective-permute-start(bf16[4,10,1,256]{3,2,1,0:T(2,128)(2,1)S(1)} %get-tuple-element.108), channel_id=1, source_target_pairs={{2,0},{4,2},{6,4},{8,6},{10,8},{12,10},{14,12},{0,14},{3,1},{5,3},... | collective-permute-start | bytes 61448 | tf_op jit(solution)/shard_map/ppermute | solution.py:23
  271.4 1.9 collective-permute-done.18
  279.3 32.5 %all-reduce = (f32[4,32]{1,0:T(4,128)S(1)}, f32[4,32]{1,0:T(4,128)S(1)}) all-reduce(f32[4,32]{1,0:T(4,128)S(1)} %copy.51, f32[4,32]{1,0:T(4,128)S(1)} %copy.50), channel_id=1, replica_groups=mesh['groups'=2,'blk'=8,'rows'=2] {'blk','rows'}, use_global_device_ids=true, to_apply=%region_25.26 | all-reduce | flops 256 | bytes 2048 | tf_op jit(solution)/shard_map/psum | solution.py:46
  315.2 1.8 collective-permute-done.21
  317.2 4.7 %collective-permute-start.23 = (bf16[4,10,1,256]{3,2,1,0:T(2,128)(2,1)S(1)}, bf16[4,10,1,256]{3,2,1,0:T(2,128)(2,1)S(1)}, u32[]{:S(2)}, u32[]{:S(2)}) collective-permute-start(bf16[4,10,1,256]{3,2,1,0:T(2,128)(2,1)S(1)} %get-tuple-element.104), channel_id=1, source_target_pairs={{2,0},{4,2},{6,4},{8,6},{10,8},{12,10},{14,12},{0,14},{3,1},{5,3},... | collective-permute-start | bytes 61448 | tf_op jit(solution)/shard_map/ppermute | solution.py:23
  321.9 2.0 collective-permute-done.22
  (225 shorter events, 74.8 us)
Async XLA Ops:
  38.2 8.4 %collective-permute-start = (bf16[4,1,32,512]{3,2,1,0:T(8,128)(2,1)S(1)}, bf16[4,1,32,512]{3,2,1,0:T(8,128)(2,1)S(1)}, u32[]{:S(2)}, u32[]{:S(2)}) collective-permute-start(bf16[4,1,32,512]{3,2,1,0:T(8,128)(2,1)S(1)} %get-tuple-element.69), channel_id=1, source_target_pairs={{0,1},{2,3},{4,5},{6,7},{8,9},{10,11},{12,13},{14,15},{16,17},{18,... | collective-permute-start | bytes 393224 | tf_op jit(solution)/shard_map/ppermute | solution.py:20
  39.7 6.9 %collective-permute-start.1 = (bf16[4,1,32,512]{3,2,1,0:T(8,128)(2,1)S(1)}, bf16[4,1,32,512]{3,2,1,0:T(8,128)(2,1)S(1)}, u32[]{:S(2)}, u32[]{:S(2)}) collective-permute-start(bf16[4,1,32,512]{3,2,1,0:T(8,128)(2,1)S(1)} %get-tuple-element.70), channel_id=1, source_target_pairs={{1,0},{3,2},{5,4},{7,6},{9,8},{11,10},{13,12},{15,14},{17,16},{19,... | collective-permute-start | bytes 393224 | tf_op jit(solution)/shard_map/ppermute | solution.py:23
  47.4 8.2 %collective-permute-start.2 = (bf16[4,10,1,512]{3,2,1,0:T(2,128)(2,1)}, bf16[4,10,1,512]{3,2,1,0:T(2,128)(2,1)}, u32[]{:S(2)}, u32[]{:S(2)}) collective-permute-start(bf16[4,10,1,512]{3,2,1,0:T(2,128)(2,1)} %get-tuple-element.64), channel_id=1, source_target_pairs={{0,2},{2,4},{4,6},{6,8},{8,10},{10,12},{12,14},{14,0},{1,3},{3,5},... | collective-permute-start | bytes 122888 | tf_op jit(solution)/shard_map/ppermute | solution.py:20
  47.4 8.2 %collective-permute-start.3 = (bf16[4,10,1,512]{3,2,1,0:T(2,128)(2,1)S(1)}, bf16[4,10,1,512]{3,2,1,0:T(2,128)(2,1)}, u32[]{:S(2)}, u32[]{:S(2)}) collective-permute-start(bf16[4,10,1,512]{3,2,1,0:T(2,128)(2,1)S(1)} %get-tuple-element.65), channel_id=1, source_target_pairs={{2,0},{4,2},{6,4},{8,6},{10,8},{12,10},{14,12},{0,14},{3,1},{5,3},... | collective-permute-start | bytes 122888 | tf_op jit(solution)/shard_map/ppermute | solution.py:23
  100.8 3.1 collective-permute-start.4
  102.1 3.1 collective-permute-start.5
  105.3 6.8 %collective-permute-start.6 = (bf16[4,10,1,256]{3,2,1,0:T(2,128)(2,1)S(1)}, bf16[4,10,1,256]{3,2,1,0:T(2,128)(2,1)S(1)}, u32[]{:S(2)}, u32[]{:S(2)}) collective-permute-start(bf16[4,10,1,256]{3,2,1,0:T(2,128)(2,1)S(1)} %get-tuple-element.119), channel_id=1, source_target_pairs={{0,2},{2,4},{4,6},{6,8},{8,10},{10,12},{12,14},{14,0},{1,3},{3,5},... | collective-permute-start | bytes 61448 | tf_op jit(solution)/shard_map/ppermute | solution.py:20
  105.4 6.7 %collective-permute-start.7 = (bf16[4,10,1,256]{3,2,1,0:T(2,128)(2,1)S(1)}, bf16[4,10,1,256]{3,2,1,0:T(2,128)(2,1)S(1)}, u32[]{:S(2)}, u32[]{:S(2)}) collective-permute-start(bf16[4,10,1,256]{3,2,1,0:T(2,128)(2,1)S(1)} %get-tuple-element.120), channel_id=1, source_target_pairs={{2,0},{4,2},{6,4},{8,6},{10,8},{12,10},{14,12},{0,14},{3,1},{5,3},... | collective-permute-start | bytes 61448 | tf_op jit(solution)/shard_map/ppermute | solution.py:23
  155.4 2.6 collective-permute-start.8
  156.7 3.1 collective-permute-start.9
  160.0 6.8 %collective-permute-start.10 = (bf16[4,10,1,256]{3,2,1,0:T(2,128)(2,1)S(1)}, bf16[4,10,1,256]{3,2,1,0:T(2,128)(2,1)S(1)}, u32[]{:S(2)}, u32[]{:S(2)}) collective-permute-start(bf16[4,10,1,256]{3,2,1,0:T(2,128)(2,1)S(1)} %get-tuple-element.115), channel_id=1, source_target_pairs={{0,2},{2,4},{4,6},{6,8},{8,10},{10,12},{12,14},{14,0},{1,3},{3,5},... | collective-permute-start | bytes 61448 | tf_op jit(solution)/shard_map/ppermute | solution.py:20
  160.0 6.7 %collective-permute-start.11 = (bf16[4,10,1,256]{3,2,1,0:T(2,128)(2,1)S(1)}, bf16[4,10,1,256]{3,2,1,0:T(2,128)(2,1)S(1)}, u32[]{:S(2)}, u32[]{:S(2)}) collective-permute-start(bf16[4,10,1,256]{3,2,1,0:T(2,128)(2,1)S(1)} %get-tuple-element.116), channel_id=1, source_target_pairs={{2,0},{4,2},{6,4},{8,6},{10,8},{12,10},{14,12},{0,14},{3,1},{5,3},... | collective-permute-start | bytes 61448 | tf_op jit(solution)/shard_map/ppermute | solution.py:23
  208.2 2.6 collective-permute-start.12
  209.5 3.1 collective-permute-start.13
  212.7 6.8 %collective-permute-start.14 = (bf16[4,10,1,256]{3,2,1,0:T(2,128)(2,1)S(1)}, bf16[4,10,1,256]{3,2,1,0:T(2,128)(2,1)S(1)}, u32[]{:S(2)}, u32[]{:S(2)}) collective-permute-start(bf16[4,10,1,256]{3,2,1,0:T(2,128)(2,1)S(1)} %get-tuple-element.111), channel_id=1, source_target_pairs={{0,2},{2,4},{4,6},{6,8},{8,10},{10,12},{12,14},{14,0},{1,3},{3,5},... | collective-permute-start | bytes 61448 | tf_op jit(solution)/shard_map/ppermute | solution.py:20
  212.8 6.7 %collective-permute-start.15 = (bf16[4,10,1,256]{3,2,1,0:T(2,128)(2,1)S(1)}, bf16[4,10,1,256]{3,2,1,0:T(2,128)(2,1)S(1)}, u32[]{:S(2)}, u32[]{:S(2)}) collective-permute-start(bf16[4,10,1,256]{3,2,1,0:T(2,128)(2,1)S(1)} %get-tuple-element.112), channel_id=1, source_target_pairs={{2,0},{4,2},{6,4},{8,6},{10,8},{12,10},{14,12},{0,14},{3,1},{5,3},... | collective-permute-start | bytes 61448 | tf_op jit(solution)/shard_map/ppermute | solution.py:23
  262.0 2.6 collective-permute-start.16
  263.3 3.1 collective-permute-start.17
  266.5 6.8 %collective-permute-start.18 = (bf16[4,10,1,256]{3,2,1,0:T(2,128)(2,1)S(1)}, bf16[4,10,1,256]{3,2,1,0:T(2,128)(2,1)S(1)}, u32[]{:S(2)}, u32[]{:S(2)}) collective-permute-start(bf16[4,10,1,256]{3,2,1,0:T(2,128)(2,1)S(1)} %get-tuple-element.107), channel_id=1, source_target_pairs={{0,2},{2,4},{4,6},{6,8},{8,10},{10,12},{12,14},{14,0},{1,3},{3,5},... | collective-permute-start | bytes 61448 | tf_op jit(solution)/shard_map/ppermute | solution.py:20
  266.6 6.7 %collective-permute-start.19 = (bf16[4,10,1,256]{3,2,1,0:T(2,128)(2,1)S(1)}, bf16[4,10,1,256]{3,2,1,0:T(2,128)(2,1)S(1)}, u32[]{:S(2)}, u32[]{:S(2)}) collective-permute-start(bf16[4,10,1,256]{3,2,1,0:T(2,128)(2,1)S(1)} %get-tuple-element.108), channel_id=1, source_target_pairs={{2,0},{4,2},{6,4},{8,6},{10,8},{12,10},{14,12},{0,14},{3,1},{5,3},... | collective-permute-start | bytes 61448 | tf_op jit(solution)/shard_map/ppermute | solution.py:23
  312.6 2.6 collective-permute-start.20
  313.9 3.1 collective-permute-start.21
  317.1 6.8 %collective-permute-start.22 = (bf16[4,10,1,256]{3,2,1,0:T(2,128)(2,1)S(1)}, bf16[4,10,1,256]{3,2,1,0:T(2,128)(2,1)S(1)}, u32[]{:S(2)}, u32[]{:S(2)}) collective-permute-start(bf16[4,10,1,256]{3,2,1,0:T(2,128)(2,1)S(1)} %get-tuple-element.103), channel_id=1, source_target_pairs={{0,2},{2,4},{4,6},{6,8},{8,10},{10,12},{12,14},{14,0},{1,3},{3,5},... | collective-permute-start | bytes 61448 | tf_op jit(solution)/shard_map/ppermute | solution.py:20
  317.2 6.7 %collective-permute-start.23 = (bf16[4,10,1,256]{3,2,1,0:T(2,128)(2,1)S(1)}, bf16[4,10,1,256]{3,2,1,0:T(2,128)(2,1)S(1)}, u32[]{:S(2)}, u32[]{:S(2)}) collective-permute-start(bf16[4,10,1,256]{3,2,1,0:T(2,128)(2,1)S(1)} %get-tuple-element.104), channel_id=1, source_target_pairs={{2,0},{4,2},{6,4},{8,6},{10,8},{12,10},{14,12},{0,14},{3,1},{5,3},... | collective-permute-start | bytes 61448 | tf_op jit(solution)/shard_map/ppermute | solution.py:23
  (31 other events, 347.8 us)
where the time goes:
time: 331 us; the launch traced here: 330 us
  blocking collectives  199 us (60%)
  starting transfers between devices  44.3 us (13%)
  local copies, waits for them, and re-layouts  31.8 us (10%)
  other arithmetic  21.7 us (7%)
  waiting for transfers between devices  19.8 us (6%)
  matrix products  12.2 us (4%)
    psum x6, blocking collectives, norm_act(): lax.psum((group_totals(inner, GROUPS), group_totals(inner * inner, GROUPS...  199 us
    ppermute x12, starting transfers between devices, with_halo(): lax.ppermute(lax.slice_in_dim(block, 0, width, axis=dim), axis, backward)  36 us
    dot_general x18, matrix products, convolve(): jnp.dot(stacked.reshape(-1, 3 * inputs), weight[shift_row].reshape(3 * in...  11.8 us
    ppermute x12, waiting for transfers between devices, with_halo(): lax.ppermute(lax.slice_in_dim(block, block.shape[dim] - width, None, axis...  11.1 us
    ppermute x12, waiting for transfers between devices, with_halo(): lax.ppermute(lax.slice_in_dim(block, 0, width, axis=dim), axis, backward)  8.75 us
    ppermute x12, starting transfers between devices, with_halo(): lax.ppermute(lax.slice_in_dim(block, block.shape[dim] - width, None, axis...  8.32 us
    reduce_sum x8, other arithmetic, group_totals(): return jnp.sum(shaped, axis=(1, 3))  7.68 us
    reshape x5, local copies, waits for them, and re-layouts, convolve(): return total.reshape(padded.shape[0], height, width, weight.shape[3]) + bias  7.09 us
  transfers between devices with their start and end apart: 24, of which 11 were waited for; matrix products, arithmetic and copies ran while one was open for 2% of the time, Pallas kernels for 0%

commit v1 on v0

v1 whole, which is shorter than its diff:
```python
import functools

import jax
import jax.numpy as jnp
from jax import lax
from jax.experimental import pallas as pl
from jax.experimental.pallas import tpu as pltpu
from jax.sharding import PartitionSpec as P

GROUPS = 32
RESNETS = 3
STAGES = 2 * RESNETS
LANES = 128
EPS = 1e-06
MESH = pl.DeviceIdType.MESH


def lane_group_sum(rows, size):
    lane = lax.broadcasted_iota(jnp.int32, rows.shape, 1)
    step = 1
    while step < size:
        ahead = pltpu.roll(rows, LANES - step, 1)
        behind = pltpu.roll(rows, step, 1)
        rows = rows + jnp.where((lane & step) == 0, ahead, behind)
        step *= 2
    return rows


def slot_mask(size):
    lane = lax.broadcasted_iota(jnp.int32, (8, LANES), 1)
    sub = lax.broadcasted_iota(jnp.int32, (8, LANES), 0)
    return (lane & (size - 1)) == sub


def kernel(
    nblk,
    nrow,
    features,
    gain_in,
    shift_in,
    conv_first,
    bias_first,
    short_weight,
    short_bias,
    gains_rest,
    shifts_rest,
    convs_rest,
    biases_rest,
    out,
    feat,
    g0,
    h0,
    w0,
    b0,
    sw,
    sb,
    gr,
    hr,
    wr,
    br,
    inner,
    stream,
    skip,
    act0,
    act1,
    rows0,
    rows1,
    cols0,
    cols1,
    corn0,
    corn1,
    scol0,
    scol1,
    scor0,
    scor1,
    stats,
    load_sem,
    out_sem,
    send_sem,
    recv_sem,
):
    images, height, width, cin = feat.shape
    ch = stream.shape[3]
    ndev = nblk * nrow
    blk = lax.axis_index("blk")
    row = lax.axis_index("rows")
    me = blk * nrow + row
    right = lax.rem(blk + 1, nblk)
    left = lax.rem(blk + nblk - 1, nblk)
    other = 1 - row
    edge = (height - 1) * other
    halo_at = (height + 1) * other
    zero_at = (height + 1) * row

    def device(k):
        target = lax.rem(me + k, ndev)
        return {"blk": target // nrow, "rows": lax.rem(target, nrow)}

    barrier = pltpu.get_barrier_semaphore()

    def greet(k, carry):
        pl.semaphore_signal(barrier, inc=1, device_id=device(k), device_id_type=MESH)
        return carry

    lax.fori_loop(1, ndev, greet, 0)

    loads = []

    def load(src, dst):
        copy = pltpu.make_async_copy(src, dst, load_sem.at[len(loads)])
        copy.start()
        loads.append(copy)
        return copy

    load_feat = [load(features.at[i], feat.at[i]) for i in range(images)]
    load_small = [
        load(a, b)
        for a, b in (
            (gain_in, g0),
            (shift_in, h0),
            (bias_first, b0),
            (short_bias, sb),
            (gains_rest, gr),
            (shifts_rest, hr),
            (biases_rest, br),
        )
    ]
    load_short = load(short_weight, sw)
    load_conv = [load(conv_first, w0)]
    for s in range(1, STAGES):
        load_conv.append(load(convs_rest.at[s - 1], wr.at[s - 1]))

    def transfers(s, i, source):
        if s == 0:
            rbuf, cbuf, nbuf = rows0.at[i], cols0.at[i], corn0.at[i]
            sc, sn = scol0.at[i], scor0.at[i]
        else:
            rbuf, cbuf, nbuf = rows1.at[s - 1, i], cols1.at[s - 1, i], corn1.at[s - 1, i]
            sc, sn = scol1.at[s - 1, i], scor1.at[s - 1, i]

        def remote(src, dst, kind, to):
            return pltpu.make_async_remote_copy(
                src_ref=src,
                dst_ref=dst,
                send_sem=send_sem.at[kind, s, i],
                recv_sem=recv_sem.at[kind, s, i],
                device_id=to,
                device_id_type=MESH,
            )

        halo = [
            remote(source.at[i, edge], rbuf, 0, {"rows": other}),
            remote(sc.at[1], cbuf.at[0], 1, {"blk": right}),
            remote(sc.at[0], cbuf.at[1], 1, {"blk": left}),
            remote(sn.at[1], nbuf.at[0], 2, {"blk": right, "rows": other}),
            remote(sn.at[0], nbuf.at[1], 2, {"blk": left, "rows": other}),
        ]
        mine = stats.at[s, i, me]

        def stat(k):
            return remote(mine, mine, 3, device(k))

        part = stats.at[s, i, pl.ds(0, ndev - 1)]
        waits = [
            remote(source.at[i, edge], rbuf, 0, {"rows": other}),
            remote(sc, cbuf, 1, {"blk": right}),
            remote(sn, nbuf, 2, {"blk": right, "rows": other}),
            remote(part, part, 3, {"rows": other}),
        ]
        return halo, stat, waits

    def publish(s, i, source, values):
        channels = values.shape[1]
        blocks = channels // LANES
        size = channels // GROUPS
        sc = scol0.at[i] if s == 0 else scol1.at[s - 1, i]
        sn = scor0.at[i] if s == 0 else scor1.at[s - 1, i]
        total = jnp.sum(values, axis=0, keepdims=True)
        square = jnp.sum(values * values, axis=0, keepdims=True)
        for r in range(height):
            sc[0, r : r + 1, :] = values[r * width : r * width + 1]
            sc[1, r : r + 1, :] = values[(r + 1) * width - 1 : (r + 1) * width]
        last = (height - 1) * width
        top = jnp.full((1, channels), row, jnp.int32) == 1
        sn[0] = jnp.where(top, values[0:1], values[last : last + 1])
        sn[1] = jnp.where(top, values[width - 1 : width], values[last + width - 1 : last + width])
        pieces = [total[:, b * LANES : (b + 1) * LANES] for b in range(blocks)]
        pieces += [square[:, b * LANES : (b + 1) * LANES] for b in range(blocks)]
        if len(pieces) < 8:
            pieces.append(jnp.zeros((8 - len(pieces), LANES), jnp.float32))
        table = lane_group_sum(jnp.concatenate(pieces, axis=0), size)
        packed = jnp.sum(jnp.where(slot_mask(size), table, 0.0), axis=0, keepdims=True)
        stats[s, i, me] = packed
        return transfers(s, i, source)

    def start(moves):
        halo, stat, _ = moves

        def one(k, carry):
            stat(k).start()
            return carry

        lax.fori_loop(1, ndev, one, 0)
        for copy in halo:
            copy.start()

    def coefficients(s, i, channels, gain, shift):
        blocks = channels // LANES
        size = channels // GROUPS
        count = height * width * ndev * size
        total = jnp.sum(stats[s, i], axis=0)
        table = jnp.where(slot_mask(size), jnp.broadcast_to(total, (8, LANES)), 0.0)
        table = lane_group_sum(table, size) * (1.0 / count)
        center = jnp.concatenate([table[b : b + 1] for b in range(blocks)], axis=1)
        square = jnp.concatenate([table[blocks + b : blocks + b + 1] for b in range(blocks)], axis=1)
        scale = 0.5 * lax.rsqrt(square - center * center + EPS) * gain
        return scale, 0.5 * shift - center * scale

    def activate(s, i, source, gain, shift):
        channels = source.shape[3]
        act = act0 if s == 0 else act1
        rbuf = rows0.at[i] if s == 0 else rows1.at[s - 1, i]
        cbuf = cols0.at[i] if s == 0 else cols1.at[s - 1, i]
        nbuf = corn0.at[i] if s == 0 else corn1.at[s - 1, i]
        scale, offset = coefficients(s, i, channels, gain, shift)

        def silu(x):
            half = x.astype(jnp.float32) * scale + offset
            return half + half * jnp.tanh(half)

        line = lax.broadcasted_iota(jnp.int32, (width, channels), 0)

        def put(at, x, low, high):
            y = silu(x)
            act[at, :, 0:channels] = jnp.where(line == 0, low, pltpu.roll(y, 1, 0)).astype(jnp.bfloat16)
            act[at, :, channels : 2 * channels] = y.astype(jnp.bfloat16)
            act[at, :, 2 * channels : 3 * channels] = jnp.where(
                line == width - 1, high, pltpu.roll(y, width - 1, 0)
            ).astype(jnp.bfloat16)

        low = silu(cbuf[0])
        high = silu(cbuf[1])
        for r in range(height):
            put(r + 1, source[i, r], low[r : r + 1], high[r : r + 1])
        put(halo_at, rbuf[...], silu(nbuf[0]), silu(nbuf[1]))

    def convolve(s):
        act = act0 if s == 0 else act1
        weight = w0[...] if s == 0 else wr[s - 1]
        taps = act.shape[2]
        field = jnp.concatenate(
            [act[d : d + height].reshape(height * width, taps) for d in range(3)], axis=1
        )
        return jnp.dot(field, weight, preferred_element_type=jnp.float32)

    act0[zero_at] = jnp.zeros(act0.shape[1:], act0.dtype)
    act1[zero_at] = jnp.zeros(act1.shape[1:], act1.dtype)

    for i in range(images):
        load_feat[i].wait()
        moves = publish(0, i, feat, feat[i].reshape(height * width, cin).astype(jnp.float32))
        if i == 0:
            pl.semaphore_wait(barrier, ndev - 1)
        start(moves)

    for copy in load_small:
        copy.wait()
    load_short.wait()

    def shortcut(i, carry):
        flat = feat[i].reshape(height * width, cin)
        skip[i] = jnp.dot(flat, sw[...], preferred_element_type=jnp.float32) + sb[...]
        return carry

    lax.fori_loop(0, images, shortcut, 0)

    for s in range(STAGES):
        load_conv[s].wait()
        source = feat if s == 0 else (inner if s % 2 == 1 else stream)
        target = inner if s % 2 == 0 else stream

        def step(i, carry, s=s, source=source, target=target):
            for copy in transfers(s, i, source)[2]:
                copy.wait()
            if s == 0:
                gain, shift, bias = g0[...], h0[...], b0[...]
            else:
                gain, shift, bias = gr[s - 1 : s], hr[s - 1 : s], br[s - 1 : s]
            activate(s, i, source, gain, shift)
            value = convolve(s) + bias
            if s == 1:
                value = value + skip[i]
            elif s % 2 == 1:
                value = value + stream[i].reshape(height * width, ch).astype(jnp.float32)
            rounded = value.astype(jnp.bfloat16)
            target[i] = rounded.reshape(height, width, ch)
            if s + 1 < STAGES:
                start(publish(s + 1, i, target, rounded.astype(jnp.float32)))
            else:
                pltpu.make_async_copy(stream.at[i], out.at[i], out_sem.at[i]).start()
            return carry

        lax.fori_loop(0, images, step, 0)

    for i in range(images):
        pltpu.make_async_copy(stream.at[i], out.at[i], out_sem.at[i]).wait()


def body(nblk, nrow, features, gain_in, shift_in, conv_first, bias_first, short_weight,
         short_bias, gains_rest, shifts_rest, convs_rest, biases_rest):
    images, height, width, cin = features.shape
    ch = conv_first.shape[3]
    rest = STAGES - 1
    ndev = nblk * nrow
    f32, bf16 = jnp.float32, jnp.bfloat16
    args = (
        features,
        gain_in.reshape(1, cin),
        shift_in.reshape(1, cin),
        conv_first.reshape(9 * cin, ch),
        bias_first.reshape(1, ch),
        short_weight,
        short_bias.reshape(1, ch),
        gains_rest,
        shifts_rest,
        convs_rest.reshape(rest, 9 * ch, ch),
        biases_rest,
    )
    anywhere = pl.BlockSpec(memory_space=pl.ANY)
    scratch = [pltpu.VMEM(a.shape, a.dtype) for a in args]
    scratch += [
        pltpu.VMEM((images, height, width, ch), bf16),
        pltpu.VMEM((images, height, width, ch), bf16),
        pltpu.VMEM((images, height * width, ch), f32),
        pltpu.VMEM((height + 2, width, 3 * cin), bf16),
        pltpu.VMEM((height + 2, width, 3 * ch), bf16),
        pltpu.VMEM((images, width, cin), bf16),
        pltpu.VMEM((rest, images, width, ch), bf16),
        pltpu.VMEM((images, 2, height, cin), f32),
        pltpu.VMEM((rest, images, 2, height, ch), f32),
        pltpu.VMEM((images, 2, 1, cin), f32),
        pltpu.VMEM((rest, images, 2, 1, ch), f32),
        pltpu.VMEM((images, 2, height, cin), f32),
        pltpu.VMEM((rest, images, 2, height, ch), f32),
        pltpu.VMEM((images, 2, 1, cin), f32),
        pltpu.VMEM((rest, images, 2, 1, ch), f32),
        pltpu.VMEM((STAGES, images, ndev, 1, LANES), f32),
        pltpu.SemaphoreType.DMA((images + 8 + STAGES,)),
        pltpu.SemaphoreType.DMA((images,)),
        pltpu.SemaphoreType.DMA((4, STAGES, images)),
        pltpu.SemaphoreType.DMA((4, STAGES, images)),
    ]
    return pl.pallas_call(
        functools.partial(kernel, nblk, nrow),
        out_shape=jax.ShapeDtypeStruct((images, height, width, ch), bf16),
        in_specs=[anywhere] * len(args),
        out_specs=anywhere,
        scratch_shapes=scratch,
        compiler_params=pltpu.CompilerParams(
            collective_id=0, has_side_effects=True, vmem_limit_bytes=48 * 1024 * 1024
        ),
    )(*args)


def solution(mesh):
    nblk, nrow = mesh.shape["blk"], mesh.shape["rows"]
    assert nrow == 2
    placed = (P("groups", "rows", "blk", None),) + (P(),) * 10
    return jax.shard_map(
        functools.partial(body, nblk, nrow),
        mesh=mesh,
        in_specs=placed,
        out_specs=P("groups", "rows", "blk", None),
        check_vma=False,
    )
```

time: 331 us -> 54.3 us (0.16)
  blocking collectives: 199 us -> 0 us
  Pallas kernels: 0 us -> 44.4 us
  starting transfers between devices: 44.3 us -> 0 us
  local copies, waits for them, and re-layouts: 31.8 us -> 9.44 us
  other arithmetic: 21.7 us -> 0 us
  waiting for transfers between devices: 19.8 us -> 0 us
  matrix products: 12.2 us -> 0 us
    psum x6 -> x0, blocking collectives: 199 us -> none  [norm_act(): lax.psum((group_totals(inner, GROUPS), group_totals(inner * inner, GROUPS...]
    pallas_call x0 -> x1, Pallas kernels: none -> 44.4 us  [body(): pl.pallas_call(functools.partial(kernel, nblk, nrow), out_shape=jax.Shape...]
    ppermute x24 -> x0, starting transfers between devices: 44.3 us -> none  [the longest x12 36 us: with_halo(): lax.ppermute(lax.slice_in_dim(block, 0, width, axis=dim), axis, backward)]
    ppermute x24 -> x0, waiting for transfers between devices: 19.8 us -> none  [the longest x12 11.1 us: with_halo(): lax.ppermute(lax.slice_in_dim(block, block.shape[dim] - width, None, axis...]
    dot_general x19 -> x0, matrix products: 12.2 us -> none  [the longest x18 11.8 us: convolve(): jnp.dot(stacked.reshape(-1, 3 * inputs), weight[shift_row].reshape(3 * in...]
    slice x22 -> x0, local copies, waits for them, and re-layouts: 9.41 us -> none  [the longest x2 5.51 us: convolve(): weight[shift_row].reshape(3 * inputs, weight.shape[3])]
    reshape x6 -> x0, local copies, waits for them, and re-layouts: 8.56 us -> none  [the longest x5 7.09 us: convolve(): return total.reshape(padded.shape[0], height, width, weight.shape[3]) + bias]
    reduce_sum x8 -> x0, other arithmetic: 7.68 us -> none  [group_totals(): return jnp.sum(shaped, axis=(1, 3))]
  transfers between devices with their start and end apart: 24 -> 0, of which waited for: 11 -> 0; matrix products, arithmetic and copies ran while one was open for 2% -> 0% of each run, Pallas kernels for 0% -> 0%
where the time goes in v1:
time: 54.3 us; the launch traced here: 53.9 us
  Pallas kernels  44.4 us (82%)
  local copies, waits for them, and re-layouts  9.44 us (17%)
    pallas_call x1, Pallas kernels, body(): pl.pallas_call(functools.partial(kernel, nblk, nrow), out_shape=jax.Shape...  44.4 us
    unnamed x21, local copies, waits for them, and re-layouts  9.44 us

profile of v1, /device:TPU:0, one launch (start us, length us, event | category | flops | bytes accessed | tf_op | source)
XLA Modules:
  0.0 53.9 jit_solution(14240705078899251999)
XLA Ops:
  0.0 0.0 copy-start
  0.0 1.7 %copy-done = bf16[3,3,512,256]{3,2,1,0:T(8,128)(2,1)S(1)} copy-done((bf16[3,3,512,256]{3,2,1,0:T(8,128)(2,1)S(1)}, bf16[3,3,512,256]{3,2,1,0:T(8,128)(2,1)}, u32[]{:S(2)}) %copy-start) | copy-done | bytes 2359320
  1.7 0.0 copy-start.1
  1.7 1.2 %copy-done.1 = bf16[4,8,32,512]{3,2,1,0:T(8,128)(2,1)S(1)} copy-done((bf16[4,8,32,512]{3,2,1,0:T(8,128)(2,1)S(1)}, bf16[4,8,32,512]{3,2,1,0:T(8,128)(2,1)}, u32[]{:S(2)}) %copy-start.1) | copy-done | bytes 1048600
  2.9 0.0 copy-start.2
  2.9 0.9 %copy-done.2 = bf16[512,256]{1,0:T(8,128)(2,1)S(1)} copy-done((bf16[512,256]{1,0:T(8,128)(2,1)S(1)}, bf16[512,256]{1,0:T(8,128)(2,1)}, u32[]{:S(2)}) %copy-start.2) | copy-done | bytes 262168
  3.8 0.0 copy-start.3
  3.8 0.7 %copy-done.3 = f32[5,256]{1,0:T(8,128)S(1)} copy-done((f32[5,256]{1,0:T(8,128)S(1)}, f32[5,256]{1,0:T(8,128)}, u32[]{:S(2)}) %copy-start.3) | copy-done | bytes 5144
  4.5 0.0 copy-start.4
  4.5 0.7 %copy-done.4 = f32[5,256]{1,0:T(8,128)S(1)} copy-done((f32[5,256]{1,0:T(8,128)S(1)}, f32[5,256]{1,0:T(8,128)}, u32[]{:S(2)}) %copy-start.4) | copy-done | bytes 5144
  5.2 0.0 copy-start.5
  5.2 0.7 %copy-done.5 = f32[5,256]{1,0:T(8,128)S(1)} copy-done((f32[5,256]{1,0:T(8,128)S(1)}, f32[5,256]{1,0:T(8,128)}, u32[]{:S(2)}) %copy-start.5) | copy-done | bytes 5144
  5.9 0.0 copy-start.6
  5.9 0.7 %copy-done.6 = f32[512]{0:T(512)S(1)} copy-done((f32[512]{0:T(512)S(1)}, f32[512]{0:T(512)}, u32[]{:S(2)}) %copy-start.6) | copy-done | bytes 2072
  6.6 0.0 copy-start.7
  6.6 0.7 %copy-done.7 = f32[512]{0:T(512)S(1)} copy-done((f32[512]{0:T(512)S(1)}, f32[512]{0:T(512)}, u32[]{:S(2)}) %copy-start.7) | copy-done | bytes 2072
  7.3 0.0 copy-start.8
  7.3 0.7 %copy-done.8 = f32[256]{0:T(256)S(1)} copy-done((f32[256]{0:T(256)S(1)}, f32[256]{0:T(256)}, u32[]{:S(2)}) %copy-start.8) | copy-done | bytes 1048
  8.0 0.0 copy-start.9
  8.0 0.7 %copy-done.9 = f32[256]{0:T(256)S(1)} copy-done((f32[256]{0:T(256)S(1)}, f32[256]{0:T(256)}, u32[]{:S(2)}) %copy-start.9) | copy-done | bytes 1048
  8.7 44.4 %shard_map.109 = bf16[4,8,32,256]{3,2,1,0:T(8,128)(2,1)S(1)} custom-call(bf16[4,8,32,512]{3,2,1,0:T(8,128)(2,1)S(1)} %copy-done.1, f32[1,512]{1,0:T(1,128)S(1)} %bitcast.7, f32[1,512]{1,0:T(1,128)S(1)} %bitcast.8, bf16[4608,256]{1,0:T(8,128)(2,1)S(1)} %bitcast.6, f32[1,256]{1,0:T(1,128)S(1)} %bitcast.9, bf16[512,256]{1,0:T(8,128)(2,1)S(1)} %copy-done.2, ...), custom_call_target="tpu_custom_call" | custom-call | tf_op jit(solution)/shard_map/pallas_call | solution.py:353
  53.1 0.8 %copy.13 = bf16[4,8,32,256]{3,2,1,0:T(8,128)(2,1)} copy(bf16[4,8,32,256]{3,2,1,0:T(8,128)(2,1)S(1)} %shard_map.109) | data formatting | bytes 1048576
Async XLA Ops:
  0.0 1.7 %copy-start = (bf16[3,3,512,256]{3,2,1,0:T(8,128)(2,1)S(1)}, bf16[3,3,512,256]{3,2,1,0:T(8,128)(2,1)}, u32[]{:S(2)}) copy-start(bf16[3,3,512,256]{3,2,1,0:T(8,128)(2,1)} %param.14) | copy-start | bytes 7077892
  1.7 1.2 %copy-start.1 = (bf16[4,8,32,512]{3,2,1,0:T(8,128)(2,1)S(1)}, bf16[4,8,32,512]{3,2,1,0:T(8,128)(2,1)}, u32[]{:S(2)}) copy-start(bf16[4,8,32,512]{3,2,1,0:T(8,128)(2,1)} %features.1) | copy-start | bytes 3145732
  2.9 0.9 %copy-start.2 = (bf16[512,256]{1,0:T(8,128)(2,1)S(1)}, bf16[512,256]{1,0:T(8,128)(2,1)}, u32[]{:S(2)}) copy-start(bf16[512,256]{1,0:T(8,128)(2,1)} %short_weight.1) | copy-start | bytes 786436
  3.8 0.7 %copy-start.3 = (f32[5,256]{1,0:T(8,128)S(1)}, f32[5,256]{1,0:T(8,128)}, u32[]{:S(2)}) copy-start(f32[5,256]{1,0:T(8,128)} %gains_rest.1) | copy-start | bytes 15364
  4.5 0.7 %copy-start.4 = (f32[5,256]{1,0:T(8,128)S(1)}, f32[5,256]{1,0:T(8,128)}, u32[]{:S(2)}) copy-start(f32[5,256]{1,0:T(8,128)} %shifts_rest.1) | copy-start | bytes 15364
  5.2 0.7 %copy-start.5 = (f32[5,256]{1,0:T(8,128)S(1)}, f32[5,256]{1,0:T(8,128)}, u32[]{:S(2)}) copy-start(f32[5,256]{1,0:T(8,128)} %biases_rest.1) | copy-start | bytes 15364
  5.9 0.7 %copy-start.6 = (f32[512]{0:T(512)S(1)}, f32[512]{0:T(512)}, u32[]{:S(2)}) copy-start(f32[512]{0:T(512)} %param.12) | copy-start | bytes 6148
  6.6 0.7 %copy-start.7 = (f32[512]{0:T(512)S(1)}, f32[512]{0:T(512)}, u32[]{:S(2)}) copy-start(f32[512]{0:T(512)} %param.13) | copy-start | bytes 6148
  7.3 0.7 %copy-start.8 = (f32[256]{0:T(256)S(1)}, f32[256]{0:T(256)}, u32[]{:S(2)}) copy-start(f32[256]{0:T(256)} %param.15) | copy-start | bytes 3076
  8.0 0.7 %copy-start.9 = (f32[256]{0:T(256)S(1)}, f32[256]{0:T(256)}, u32[]{:S(2)}) copy-start(f32[256]{0:T(256)} %param.17) | copy-start | bytes 3076

commit v2 on v1

--- a/solution.py
+++ b/solution.py
@@ -89,8 +89,6 @@
     left = lax.rem(blk + nblk - 1, nblk)
     other = 1 - row
     edge = (height - 1) * other
-    halo_at = (height + 1) * other
-    zero_at = (height + 1) * row
 
     def device(k):
         target = lax.rem(me + k, ndev)
@@ -148,28 +146,33 @@
                 device_id_type=MESH,
             )
 
-        halo = [
-            remote(source.at[i, edge], rbuf, 0, {"rows": other}),
-            remote(sc.at[1], cbuf.at[0], 1, {"blk": right}),
-            remote(sc.at[0], cbuf.at[1], 1, {"blk": left}),
-            remote(sn.at[1], nbuf.at[0], 2, {"blk": right, "rows": other}),
-            remote(sn.at[0], nbuf.at[1], 2, {"blk": left, "rows": other}),
-        ]
+        def halo():
+            return [
+                remote(sc.at[1], cbuf.at[0], 1, {"blk": right}),
+                remote(sc.at[0], cbuf.at[1], 1, {"blk": left}),
+                remote(sn.at[1], nbuf.at[0], 2, {"blk": right, "rows": other}),
+                remote(sn.at[0], nbuf.at[1], 2, {"blk": left, "rows": other}),
+                remote(source.at[i, edge], rbuf, 0, {"rows": other}),
+            ]
+
         mine = stats.at[s, i, me]
 
         def stat(k):
             return remote(mine, mine, 3, device(k))
 
         part = stats.at[s, i, pl.ds(0, ndev - 1)]
-        waits = [
-            remote(source.at[i, edge], rbuf, 0, {"rows": other}),
-            remote(sc, cbuf, 1, {"blk": right}),
-            remote(sn, nbuf, 2, {"blk": right, "rows": other}),
-            remote(part, part, 3, {"rows": other}),
-        ]
+
+        def waits():
+            return [
+                remote(source.at[i, edge], rbuf, 0, {"rows": other}),
+                remote(sc, cbuf, 1, {"blk": right}),
+                remote(sn, nbuf, 2, {"blk": right, "rows": other}),
+                remote(part, part, 3, {"rows": other}),
+            ]
+
         return halo, stat, waits
 
-    def publish(s, i, source, values):
+    def publish(s, i, source, values, entry=None):
         channels = values.shape[1]
         blocks = channels // LANES
         size = channels // GROUPS
@@ -177,6 +180,19 @@
         sn = scor0.at[i] if s == 0 else scor1.at[s - 1, i]
         total = jnp.sum(values, axis=0, keepdims=True)
         square = jnp.sum(values * values, axis=0, keepdims=True)
+        pieces = [total[:, b * LANES : (b + 1) * LANES] for b in range(blocks)]
+        pieces += [square[:, b * LANES : (b + 1) * LANES] for b in range(blocks)]
+        if len(pieces) < 8:
+            pieces.append(jnp.zeros((8 - len(pieces), LANES), jnp.float32))
+        table = lane_group_sum(jnp.concatenate(pieces, axis=0), size)
+        packed = jnp.sum(jnp.where(slot_mask(size), table, 0.0), axis=0, keepdims=True)
+        stats[s, i, me] = packed
+        halo, stat, _ = transfers(s, i, source)
+        if entry is not None:
+            entry()
+
+        for k in sorted(range(1, ndev), key=lambda k: abs(k - ndev // 2)):
+            stat(k).start()
         for r in range(height):
             sc[0, r : r + 1, :] = values[r * width : r * width + 1]
             sc[1, r : r + 1, :] = values[(r + 1) * width - 1 : (r + 1) * width]
@@ -184,24 +200,7 @@
         top = jnp.full((1, channels), row, jnp.int32) == 1
         sn[0] = jnp.where(top, values[0:1], values[last : last + 1])
         sn[1] = jnp.where(top, values[width - 1 : width], values[last + width - 1 : last + width])
-        pieces = [total[:, b * LANES : (b + 1) * LANES] for b in range(blocks)]
-        pieces += [square[:, b * LANES : (b + 1) * LANES] for b in range(blocks)]
-        if len(pieces) < 8:
-            pieces.append(jnp.zeros((8 - len(pieces), LANES), jnp.float32))
-        table = lane_group_sum(jnp.concatenate(pieces, axis=0), size)
-        packed = jnp.sum(jnp.where(slot_mask(size), table, 0.0), axis=0, keepdims=True)
-        stats[s, i, me] = packed
-        return transfers(s, i, source)
-
-    def start(moves):
-        halo, stat, _ = moves
-
-        def one(k, carry):
-            stat(k).start()
-            return carry
-
-        lax.fori_loop(1, ndev, one, 0)
-        for copy in halo:
+        for copy in halo():
             copy.start()
 
     def coefficients(s, i, channels, gain, shift):
@@ -230,19 +229,25 @@
 
         line = lax.broadcasted_iota(jnp.int32, (width, channels), 0)
 
-        def put(at, x, low, high):
+        def three(x, low, high):
             y = silu(x)
-            act[at, :, 0:channels] = jnp.where(line == 0, low, pltpu.roll(y, 1, 0)).astype(jnp.bfloat16)
-            act[at, :, channels : 2 * channels] = y.astype(jnp.bfloat16)
-            act[at, :, 2 * channels : 3 * channels] = jnp.where(
-                line == width - 1, high, pltpu.roll(y, width - 1, 0)
-            ).astype(jnp.bfloat16)
+            return (
+                jnp.where(line == 0, low, pltpu.roll(y, 1, 0)),
+                y,
+                jnp.where(line == width - 1, high, pltpu.roll(y, width - 1, 0)),
+            )
 
         low = silu(cbuf[0])
         high = silu(cbuf[1])
+        outer = three(rbuf[...], silu(nbuf[0]), silu(nbuf[1]))
+        above = jnp.where(row == 1, 1.0, 0.0)
+        for d, piece in enumerate(outer):
+            at = pl.ds(d * channels, channels)
+            act[0, :, at] = (piece * above).astype(jnp.bfloat16)
+            act[height + 1, :, at] = (piece * (1.0 - above)).astype(jnp.bfloat16)
         for r in range(height):
-            put(r + 1, source[i, r], low[r : r + 1], high[r : r + 1])
-        put(halo_at, rbuf[...], silu(nbuf[0]), silu(nbuf[1]))
+            for d, piece in enumerate(three(source[i, r], low[r : r + 1], high[r : r + 1])):
+                act[r + 1, :, pl.ds(d * channels, channels)] = piece.astype(jnp.bfloat16)
 
     def convolve(s):
         act = act0 if s == 0 else act1
@@ -253,15 +258,10 @@
         )
         return jnp.dot(field, weight, preferred_element_type=jnp.float32)
 
-    act0[zero_at] = jnp.zeros(act0.shape[1:], act0.dtype)
-    act1[zero_at] = jnp.zeros(act1.shape[1:], act1.dtype)
-
     for i in range(images):
         load_feat[i].wait()
-        moves = publish(0, i, feat, feat[i].reshape(height * width, cin).astype(jnp.float32))
-        if i == 0:
-            pl.semaphore_wait(barrier, ndev - 1)
-        start(moves)
+        values = feat[i].reshape(height * width, cin).astype(jnp.float32)
+        publish(0, i, feat, values, functools.partial(pl.semaphore_wait, barrier, ndev - 1) if i == 0 else None)
 
     for copy in load_small:
         copy.wait()
@@ -280,7 +280,7 @@
         target = inner if s % 2 == 0 else stream
 
         def step(i, carry, s=s, source=source, target=target):
-            for copy in transfers(s, i, source)[2]:
+            for copy in transfers(s, i, source)[2]():
                 copy.wait()
             if s == 0:
                 gain, shift, bias = g0[...], h0[...], b0[...]
@@ -295,7 +295,7 @@
             rounded = value.astype(jnp.bfloat16)
             target[i] = rounded.reshape(height, width, ch)
             if s + 1 < STAGES:
-                start(publish(s + 1, i, target, rounded.astype(jnp.float32)))
+                publish(s + 1, i, target, rounded.astype(jnp.float32))
             else:
                 pltpu.make_async_copy(stream.at[i], out.at[i], out_sem.at[i]).start()
             return carry
@@ -357,7 +357,7 @@
         out_specs=anywhere,
         scratch_shapes=scratch,
         compiler_params=pltpu.CompilerParams(
-            collective_id=0, has_side_effects=True, vmem_limit_bytes=48 * 1024 * 1024
+            collective_id=0, has_side_effects=True, vmem_limit_bytes=67043328
         ),
     )(*args)
 

time: 54.3 us -> 45.6 us (0.84)
  local copies, waits for them, and re-layouts: 9.44 us -> 1.87 us
  Pallas kernels: 44.4 us -> 43.6 us
    unnamed x21 -> x1, local copies, waits for them, and re-layouts: 9.44 us -> 1.87 us
    pallas_call x1, Pallas kernels: 44.4 us -> 43.6 us  [body(): pl.pallas_call(functools.partial(kernel, nblk, nrow), out_shape=jax.Shape...]
where the time goes in v2:
time: 45.6 us; the launch traced here: 45.5 us
  Pallas kernels  43.6 us (96%)
  local copies, waits for them, and re-layouts  1.87 us (4%)
    pallas_call x1, Pallas kernels, body(): pl.pallas_call(functools.partial(kernel, nblk, nrow), out_shape=jax.Shape...  43.6 us
    unnamed x1, local copies, waits for them, and re-layouts  1.87 us

profile of v2, /device:TPU:0, one launch (start us, length us, event | category | flops | bytes accessed | tf_op | source)
XLA Modules:
  0.0 45.5 jit_solution(389134424915862110)
XLA Ops:
  0.0 43.6 %shard_map.109 = bf16[4,8,32,256]{3,2,1,0:T(8,128)(2,1)} custom-call(bf16[4,8,32,512]{3,2,1,0:T(8,128)(2,1)} %features.1, f32[1,512]{1,0:T(1,128)} %bitcast.8, f32[1,512]{1,0:T(1,128)} %bitcast.9, bf16[4608,256]{1,0:T(8,128)(2,1)} %bitcast.7, f32[1,256]{1,0:T(1,128)} %bitcast.10, bf16[512,256]{1,0:T(8,128)(2,1)} %short_weight.1, f32[1,256]{1,0:T(1,128)} %bitcast.11, ...), custom_call_target="tpu_custom_call" | custom-call | tf_op jit(solution)/shard_map/pallas_call | solution.py:353
  43.6 1.9 %copy.13 = bf16[4,8,32,256]{3,2,1,0:T(8,128)(2,1)} copy(bf16[4,8,32,256]{3,2,1,0:T(8,128)(2,1)} %shard_map.109) | data formatting | bytes 1048576
